TPU v7x, 32 devices: a whole 2x2x4 slice. The times are simulated.
32 devices in a mesh: row: 4 (over z), col: 8 (over y, x, core).
Axes of the slice: x: 2, y: 2, z: 4, core: 2. Of those that a mesh axis runs over, the one named last changes fastest.
Arguments:
- neighbor: int32 [32, 3072, 3072], P(None, 'col', 'row'), may hold values from 0 to 1, as said below
- true_coords: float32 [32, 3, 3072], P(None, None, ('row', 'col')), as said below
- pred_coords: float32 [32, 3, 3072], P(None, None, ('row', 'col')), as said below
- residue_mask: int32 [32, 3072], P(None, ('row', 'col')), may hold values from 0 to 1, as said below
- single: bfloat16 [32, 3072, 384], P(None, ('row', 'col'))
- ln_gain: float32 [384], replicated, may hold values from 0.1 to 1.9
- w_hidden: bfloat16 [384, 128], replicated, may hold values from -0.3125 to 0.3125
- b_hidden: float32 [128], replicated, may hold values from -3 to 3
- w_mid: bfloat16 [128, 128], replicated, may hold values from -0.5 to 0.5
- b_mid: float32 [128], replicated, may hold values from -3 to 3
- w_logits: bfloat16 [128, 50], replicated, may hold values from -1.5 to 1.5
- b_logits: float32 [50], replicated, may hold values from -4 to 4
Outputs:
- lddt_score: float32 [32, 3072], P(None, ('row', 'col'))
- residue_loss: float32 [32, 3072], P(None, ('row', 'col'))
- total_loss: float32 [], replicated
Inputs may be any that keep to these rules, and one draw needn't show every extreme that they name: `neighbor`: 0 or 1; 0 where j == i; 1 wherever 0 < |i - j| <= 8. `residue_mask`: per structure, 1 on a leading run of 1536 or more residues and 0 after it. `true_coords`: positions in angstroms. `pred_coords`: positions in angstroms.
All inputs are finite; a program needn't handle non-finite values.
Results may differ from a plain program's by a relative error of at most 0.00098.
Values sent between devices are 32-bit elements; how exact they have to be, the bound alone decides.
A program may use at most 128 MiB of HBM per device.

v0:
```python
import jax
import jax.numpy as jnp
from jax import lax
from jax.sharding import PartitionSpec as P

L = 3072


THRESHOLDS = (0.5, 1.0, 2.0, 4.0)


def from_root(shard, axis, root):
    mine = lax.axis_index(axis) == root
    return lax.psum(jnp.where(mine, shard, jnp.zeros_like(shard)), axis)


def tile_dist(rows_block, cols_block):
    total = (cols_block[:, 0, :, None] - rows_block[:, 0, None, :]) ** 2
    total = total + (cols_block[:, 1, :, None] - rows_block[:, 1, None, :]) ** 2
    total = total + (cols_block[:, 2, :, None] - rows_block[:, 2, None, :]) ** 2
    return jnp.sqrt(total + 1e-10)


def head_loss(lddt_value, single, ln_gain, w_hidden, b_hidden, w_mid, b_mid, w_logits, b_logits):
    features = single.astype(jnp.float32)
    average = jnp.mean(features, axis=-1, keepdims=True)
    centred = features - average
    variance = jnp.mean(centred * centred, axis=-1, keepdims=True)
    normed = (centred * lax.rsqrt(variance + 1e-05) * ln_gain).astype(jnp.bfloat16)
    first_hidden = jax.nn.relu(
        jnp.dot(normed, w_hidden, preferred_element_type=jnp.float32) + b_hidden
    ).astype(jnp.bfloat16)
    second_hidden = jax.nn.relu(
        jnp.dot(first_hidden, w_mid, preferred_element_type=jnp.float32) + b_mid
    ).astype(jnp.bfloat16)
    logits = jnp.dot(second_hidden, w_logits, preferred_element_type=jnp.float32) + b_logits
    log_total = jnp.log(jnp.sum(jnp.exp(logits), axis=-1))
    bins = logits.shape[-1]
    centers = (jnp.arange(bins).astype(jnp.float32) + 0.5) / bins
    closeness = jnp.exp(-((lddt_value[..., None] - centers) ** 2) * (bins * bins * 0.5))
    target = closeness / jnp.sum(closeness, axis=-1, keepdims=True)
    return log_total - jnp.sum(target * logits, axis=-1)


def local(
    neighbor,
    true_coords,
    pred_coords,
    residue_mask,
    single,
    ln_gain,
    w_hidden,
    b_hidden,
    w_mid,
    b_mid,
    w_logits,
    b_logits,
):
    valid = residue_mask.astype(jnp.float32)
    own_len = residue_mask.shape[1]
    stacked = jnp.concatenate([true_coords, pred_coords, valid[:, None, :]], axis=1)
    row_count = lax.axis_size("row")
    col_count = lax.axis_size("col")
    rows_len = L // row_count
    cols_len = L // col_count
    col_index = lax.axis_index("col")
    rows_part = lax.all_gather(stacked, "col", axis=2, tiled=True)
    offset = col_index * cols_len % rows_len
    column_piece = lax.dynamic_slice_in_dim(rows_part, offset, cols_len, 2)
    source_row = col_index * cols_len // rows_len
    cols_part = from_root(column_piece, "row", source_row)
    true_dist = tile_dist(rows_part[:, 0:3], cols_part[:, 0:3])
    pred_dist = tile_dist(rows_part[:, 3:6], cols_part[:, 3:6])
    mismatch = jnp.abs(pred_dist - true_dist)
    scores = jnp.zeros_like(mismatch)
    for threshold in THRESHOLDS:
        scores = scores + jax.nn.sigmoid(4.0 * (threshold - mismatch))
    scores = 0.25 * scores
    weights = neighbor.astype(jnp.float32) * rows_part[:, 6, None, :] * cols_part[:, 6, :, None]
    preserved = jnp.sum(weights * scores, axis=1)
    neighbors = jnp.sum(weights, axis=1)
    preserved_all, neighbors_all = lax.psum((preserved, neighbors), "col")
    preserved_own = lax.dynamic_slice_in_dim(preserved_all, col_index * own_len, own_len, 1)
    neighbors_own = lax.dynamic_slice_in_dim(neighbors_all, col_index * own_len, own_len, 1)
    lddt_score = preserved_own / jnp.maximum(neighbors_own, 1.0)
    residue_loss = valid * head_loss(
        lddt_score, single, ln_gain, w_hidden, b_hidden, w_mid, b_mid, w_logits, b_logits
    )
    loss_sum, valid_sum = lax.psum((jnp.sum(residue_loss), jnp.sum(valid)), ("row", "col"))
    total_loss = loss_sum / valid_sum
    return (lddt_score, residue_loss, total_loss)


def solution(mesh):
    placed = (
        P(None, "col", "row"),
        P(None, None, ("row", "col")),
        P(None, None, ("row", "col")),
        P(None, ("row", "col")),
        P(None, ("row", "col"), None),
        P(),
        P(),
        P(),
        P(),
        P(),
        P(),
        P(),
    )
    return jax.shard_map(
        local,
        mesh=mesh,
        in_specs=placed,
        out_specs=(P(None, ("row", "col")), P(None, ("row", "col")), P()),
        check_vma=False,
    )
```

profile of v0, /device:TPU:0, one launch (start us, length us, event | category | flops | bytes accessed | tf_op | source)
XLA Modules:
  0.0 312.7 jit_solution(15335422747212448188)
XLA Ops:
  7.2 0.0 copy-start
  7.2 0.0 all-reduce.5.cloned.1.call-start
  7.3 0.7 convert_bitcast_fusion
  8.0 0.8 pad_maximum_fusion
  8.8 0.9 copy.33
  9.7 21.3 %all_gather.3 = f32[32,7,768]{0,1,2:T(8,128)S(1)} all-gather(f32[32,7,96]{0,1,2:T(8,128)} %copy.33), channel_id=1, replica_groups=mesh['row'=4,'col'=8] {'col'}, dimensions={2}, use_global_device_ids=true | all-gather | bytes 774144 | tf_op jit(solution)/shard_map/all_gather | solution.py:67
  31.0 1.3 dynamic-slice_select_fusion
  32.3 0.0 all-reduce.5.cloned.1.call-update
  32.3 0.0 all-reduce.7.cloned.1.call-start
  32.4 3.3 %fusion.31 = (f32[32,1,768]{0,1,2:T(1,128)}, f32[32,1,768]{0,1,2:T(1,128)}, f32[32,1,768]{0,1,2:T(1,128)}, f32[32,1,768]{0,1,2:T(1,128)}, f32[32,1,768]{0,1,2:T(...) fusion(f32[32,7,768]{0,1,2:T(8,128)S(1)} %all_gather.3), kind=kLoop, calls=%fused_computation.43 | loop fusion | bytes 1376256 | tf_op jit(solution)/shard_map/slice | solution.py:79
  35.6 2.3 convert_reduce_fusion
  37.9 2.8 fusion.4
  40.8 0.0 copy-done
  40.8 3.2 %maximum_convert_fusion = bf16[32,96,128]{2,1,0:T(8,128)(2,1)S(1)} fusion(bf16[32,96,384]{2,1,0:T(8,128)(2,1)} %param.16, f32[384]{0:T(512)} %param.17, f32[32,96]{1,0:T(8,128)S(1)} %add_rsqrt_fusion, f32[32,96]{1,0:T(8,128)S(1)} %broadcast_multiply_fusion, f32[128]{0:T(128)} %param.21, f32[128]{0:T(128)} %param.19, bf16[384,128]{1,0:T(8,128)(2,1)S(1)} %copy-done, ...), kind=kOutput, calls=%fused_computation.15 | convolution fusion | flops 410910720 | bytes 3303936 | tf_op jit(solution)/shard_map/dot_general | solution.py:34
  44.0 1.1 copy.34
  45.1 1.1 copy.37
  46.2 1.1 copy.39
  47.4 1.1 copy.41
  48.5 1.1 copy.43
  49.7 1.1 copy.45
  50.8 1.1 copy.47
  51.9 1.4 exponential_reduce_fusion
  53.4 48.4 %all-reduce.5.cloned.1.call-done = f32[32,7,384]{0,1,2:T(8,128)} async-done(((f32[32,7,384]{0,1,2:T(8,128)}), f32[32,7,384]{0,1,2:T(8,128)}) %all-reduce.5.cloned.1.call-update) | async-done | bytes 344080 | tf_op jit(solution)/shard_map/psum | solution.py:14
  101.7 6.8 %fusion.32 = (f32[32,1,384]{0,1,2:T(1,128)S(1)}, f32[32,1,384]{0,1,2:T(1,128)S(1)}, f32[32,1,384]{0,1,2:T(1,128)S(1)}, f32[32,1,384]{0,1,2:T(1,128)S(1)}, f32[32...) fusion(f32[32,7,384]{0,1,2:T(8,128)} %all-reduce.5.cloned.1.call-done), kind=kLoop, calls=%fused_computation.44 | loop fusion | bytes 688128 | tf_op jit(solution)/shard_map/slice | solution.py:79
  108.5 0.1 copy.35
  108.6 0.1 copy.36
  108.7 0.1 copy.38
  108.8 0.1 copy.40
  108.9 0.1 copy.42
  109.1 0.1 copy.44
  109.2 0.1 copy.46
  109.3 0.0 copy-start.1
  109.3 98.8 %multiply_reduce_fusion = (f32[32,768]{1,0:T(8,128)}, f32[32,768]{1,0:T(8,128)}) fusion(s32[32,384,768]{2,1,0:T(8,128)} %param.12, f32[32,768]{1,0:T(8,128)S(1)} %copy.47, f32[32,384]{1,0:T(8,128)S(1)} %copy.46, f32[32,768]{1,0:T(8,128)S(1)} %copy.45, f32[32,384]{1,0:T(8,128)S(1)} %copy.44, f32[32,768]{1,0:T(8,128)S(1)} %copy.43, f32[32,384]{1,0:T(8,128)S(1)} %copy.42, ...), kind=kLoop, calls=%fused_computation.1 | loop fusion | flops 471810048 | bytes 38977536 | tf_op jit(solution)/shard_map/reduce_sum | solution.py:80
  208.1 0.0 all-reduce.7.cloned.1.call-update
  208.2 53.1 %all-reduce.7.cloned.1.call-done = (f32[32,768]{1,0:T(8,128)}, f32[32,768]{1,0:T(8,128)}) async-done(((f32[32,768]{1,0:T(8,128)}, f32[32,768]{1,0:T(8,128)}), (f32[32,768]{1,0:T(8,128)}, f32[32,768]{1,0:T(8,128)})) %all-reduce.7.cloned.1.call-update) | async-done | bytes 196624 | tf_op jit(solution)/shard_map/psum | solution.py:82
  261.3 0.9 maximum_divide_fusion
  262.1 0.0 copy-start.2
  262.1 0.4 fusion.33
  262.6 0.0 copy-done.1
  262.6 1.3 fusion.30
  263.9 39.6 %all-reduce = (f32[]{:T(128)}, f32[]{:T(128)}) all-reduce(f32[]{:T(128)} %get-tuple-element.12, f32[]{:T(128)} %get-tuple-element.28), channel_id=1, replica_groups=mesh['row'=4,'col'=8] {'row','col'}, use_global_device_ids=true, to_apply=%region_11.12 | all-reduce | flops 2 | bytes 16 | tf_op jit(solution)/shard_map/psum | solution.py:89
  304.7 0.0 copy-done.2
  (3 shorter events, 0.0 us)
Async XLA Ops:
  7.2 33.6 %copy-start = (bf16[384,128]{1,0:T(8,128)(2,1)S(1)}, bf16[384,128]{1,0:T(8,128)(2,1)}, u32[]{:S(2)}) copy-start(bf16[384,128]{1,0:T(8,128)(2,1)} %param.18) | copy-start | bytes 294916
  7.2 94.6 %all-reduce.5.cloned.1.call-start = ((), (), s32[]{:S(2)}) async-start(), calls=%async_computation | async-start | bytes 3145728 | tf_op jit(solution)/shard_map/psum | solution.py:14
  32.3 228.9 %all-reduce.7.cloned.1.call-start = ((), (), s32[]{:S(2)}) async-start(), calls=%async_computation.1 | async-start | bytes 393216 | tf_op jit(solution)/shard_map/psum | solution.py:82
  109.3 153.3 %copy-start.1 = (s32[32,96]{1,0:T(8,128)S(1)}, s32[32,96]{1,0:T(8,128)}, u32[]{:S(2)}) copy-start(s32[32,96]{1,0:T(8,128)} %param.15) | copy-start | bytes 36868
  262.1 42.6 %copy-start.2 = (f32[32,96]{1,0:T(8,128)}, f32[32,96]{1,0:T(8,128)S(1)}, u32[]{:S(2)}) copy-start(f32[32,96]{1,0:T(8,128)S(1)} %maximum_divide_fusion) | copy-start | bytes 36868
Sparse Core Ops, SparseCore 0:
  32.5 69.2 all-reduce.4
  208.3 52.9 all-reduce.6
where the time goes:
time: 314 us; the launch traced here: 313 us
  other arithmetic  109 us (35%)
  waiting for transfers between devices  102 us (32%)
  blocking collectives  60.8 us (19%)
  local copies, waits for them, and re-layouts  19.7 us (6%)
  between operations  16.6 us (5%)
  matrix products  4.59 us (1%)
    reduce_sum x1, other arithmetic, local(): preserved = jnp.sum(weights * scores, axis=1)  98.8 us
    psum x1, waiting for transfers between devices, local(): preserved_all, neighbors_all = lax.psum((preserved, neighbors), 'col')  53.1 us
    psum x1, waiting for transfers between devices, from_root(): return lax.psum(jnp.where(mine, shard, jnp.zeros_like(shard)), axis)  48.4 us
    psum x1, blocking collectives, local(): lax.psum((jnp.sum(residue_loss), jnp.sum(valid)), ('row', 'col'))  39.6 us
    all_gather x1, blocking collectives, local(): rows_part = lax.all_gather(stacked, 'col', axis=2, tiled=True)  21.3 us
    slice x1, local copies, waits for them, and re-layouts, local(): cols_part[:, 6, :, None]  6.78 us
  transfers between devices with their start and end apart: 2, of which 2 were waited for; matrix products, arithmetic and copies ran while one was open for 7% of the time, Pallas kernels for 0%

commit v1 on v0

v1 whole, which is shorter than its diff:
```python
import functools

import jax
import jax.numpy as jnp
from jax import lax
from jax.experimental import pallas as pl
from jax.experimental.pallas import tpu as pltpu
from jax.sharding import PartitionSpec as P

THRESHOLDS = (0.5, 1.0, 2.0, 4.0)
EPS = 1e-10
MESH = pl.DeviceIdType.MESH


def gather_kernel(R, C, x_ref, rows_ref, cols_ref, send_sem, recv_sem, csend_sem, crecv_sem):
    r = lax.axis_index("row")
    c = lax.axis_index("col")
    g = r * C + c
    to_col = g // R
    slot = g % R
    own = to_col == c

    barrier = pltpu.get_barrier_semaphore()
    for k in range(1, C):
        pl.semaphore_signal(barrier, inc=1, device_id=(r, (c + k) % C), device_id_type=MESH)
    for s in range(R):
        source = R * c + s

        @pl.when(source != g)
        def _():
            pl.semaphore_signal(barrier, inc=1, device_id=(source // C, source % C), device_id_type=MESH)

    pl.semaphore_wait(barrier, C - 1 + R - jnp.where(own, 1, 0))

    col_copies = []
    for k in range(1, R):
        copy = pltpu.make_async_remote_copy(
            src_ref=x_ref,
            dst_ref=cols_ref.at[slot],
            send_sem=csend_sem.at[k],
            recv_sem=crecv_sem.at[slot],
            device_id=((r + k) % R, to_col),
            device_id_type=MESH,
        )
        copy.start()
        col_copies.append(copy)
    home = pltpu.make_async_remote_copy(
        src_ref=x_ref,
        dst_ref=cols_ref.at[slot],
        send_sem=csend_sem.at[0],
        recv_sem=crecv_sem.at[slot],
        device_id=(r, to_col),
        device_id_type=MESH,
    )

    @pl.when(jnp.logical_not(own))
    def _():
        home.start()

    row_copies = []
    for k in range(1, C):
        copy = pltpu.make_async_remote_copy(
            src_ref=x_ref,
            dst_ref=rows_ref.at[c],
            send_sem=send_sem.at[k],
            recv_sem=recv_sem.at[k],
            device_id=(r, (c + k) % C),
            device_id_type=MESH,
        )
        copy.start()
        row_copies.append(copy)

    rows_ref[c] = x_ref[...]

    @pl.when(own)
    def _():
        cols_ref[slot] = x_ref[...]

    for copy in row_copies:
        copy.wait()
    for copy in col_copies:
        copy.wait_send()

    @pl.when(jnp.logical_not(own))
    def _():
        home.wait_send()

    for s in range(R):

        @pl.when(R * c + s != g)
        def _():
            pltpu.make_async_remote_copy(
                src_ref=x_ref,
                dst_ref=cols_ref.at[s],
                send_sem=csend_sem.at[0],
                recv_sem=crecv_sem.at[s],
                device_id=(r, to_col),
                device_id_type=MESH,
            ).wait_recv()


def gather(x, R, C):
    shape = x.shape
    return pl.pallas_call(
        functools.partial(gather_kernel, R, C),
        out_shape=(
            jax.ShapeDtypeStruct((C,) + shape, x.dtype),
            jax.ShapeDtypeStruct((R,) + shape, x.dtype),
        ),
        in_specs=[pl.BlockSpec(memory_space=pltpu.VMEM)],
        out_specs=[pl.BlockSpec(memory_space=pltpu.VMEM)] * 2,
        scratch_shapes=[
            pltpu.SemaphoreType.DMA((C,)),
            pltpu.SemaphoreType.DMA((C,)),
            pltpu.SemaphoreType.DMA((R,)),
            pltpu.SemaphoreType.DMA((R,)),
        ],
        compiler_params=pltpu.CompilerParams(collective_id=0, has_side_effects=True),
        name="gather",
    )(x)


def split3(x):
    first = x.astype(jnp.bfloat16).astype(jnp.float32)
    rest = x - first
    second = rest.astype(jnp.bfloat16).astype(jnp.float32)
    return first, second, rest - second


def with_norms(x, row):
    square = x * x
    true_norm = square[0:1] + square[1:2] + square[2:3]
    pred_norm = square[3:4] + square[4:5] + square[5:6]
    mixed = jnp.where(row < 6, x, jnp.where(row == 6, true_norm, pred_norm))
    return mixed, true_norm, pred_norm


def pair_kernel(
    R, C, chunk,
    rows_ref, cols_ref, neighbor_ref, single_ref, gain_ref, wh_ref, bh_ref, wm_ref, bm_ref, wl_ref, bl_ref,
    parts_ref, logits_ref, total_ref,
    left_t, left_p, right, d_true, d_pred, acc_p, acc_n,
):
    b = pl.program_id(0)
    batch = pl.num_programs(0)
    own_len = rows_ref.shape[3]
    rows_len = C * own_len
    cols_len = R * own_len
    rows = jnp.concatenate([rows_ref[s, b] for s in range(C)], axis=1)
    cols = jnp.concatenate([cols_ref[s, b] for s in range(R)], axis=1)
    keep = cols[6:7]
    center = jnp.sum(cols * keep, axis=1, keepdims=True) / jnp.maximum(jnp.sum(keep, axis=1, keepdims=True), 1.0)
    row_r = lax.broadcasted_iota(jnp.int32, rows.shape, 0)
    row_c = lax.broadcasted_iota(jnp.int32, cols.shape, 0)
    far, _, _ = with_norms((rows - center) * 2.0, row_r)
    near = (cols - center) * 2.0
    _, near_t, near_p = with_norms(near, row_c)
    f1, f2, f3 = split3(far)
    ones = jnp.ones_like(far)
    right[...] = jnp.concatenate([f1, f1, f1, f2, f2, f3, ones, jnp.zeros_like(far)], axis=0).astype(jnp.bfloat16)
    n1, n2, n3 = split3(near)
    zeros = jnp.zeros_like(near)
    for ref, low, norm_row, norm in ((left_t, 0, 6, near_t), (left_p, 3, 7, near_p)):
        inside = (row_c >= low) & (row_c < low + 3)
        l1 = jnp.where(inside, -2.0 * n1, jnp.where(row_c == norm_row, 1.0, 0.0))
        l2 = jnp.where(inside, -2.0 * n2, 0.0)
        l3 = jnp.where(inside, -2.0 * n3, 0.0)
        m1, m2, m3 = split3(norm)
        tail = jnp.where(
            row_c == 0, m1, jnp.where(row_c == 1, m2, jnp.where(row_c == 2, m3, jnp.where(row_c == 3, 4.0 * EPS, 0.0)))
        )
        side = jnp.concatenate([l1, l2, l3, l1, l2, l1, tail, zeros], axis=0)
        ref[...] = jnp.transpose(side).astype(jnp.bfloat16)
    keep_col = jnp.transpose(cols)[:, 6:7]
    width = 256
    step = 16
    for q in range(rows_len // width):
        lanes = slice(q * width, (q + 1) * width)
        half = q % 2
        weights_side = right[:, lanes]
        d_true[half] = jnp.dot(left_t[...], weights_side, preferred_element_type=jnp.float32)
        d_pred[half] = jnp.dot(left_p[...], weights_side, preferred_element_type=jnp.float32)
        total_p = jnp.zeros((8, width), jnp.float32)
        total_n = jnp.zeros((8, width), jnp.float32)
        for j in range(0, cols_len, step):
            span = slice(j, j + step)
            t2 = jnp.maximum(d_true[half, span, :], 4.0 * EPS)
            p2 = jnp.maximum(d_pred[half, span, :], 4.0 * EPS)
            gap = jnp.abs(p2 * lax.rsqrt(p2) - t2 * lax.rsqrt(t2))
            w = neighbor_ref[0, span, lanes].astype(jnp.float32) * keep_col[span]
            score = jnp.tanh(2.0 * THRESHOLDS[0] - gap)
            for threshold in THRESHOLDS[1:]:
                score = score + jnp.tanh(2.0 * threshold - gap)
            score = score * w
            for h in range(0, step, 8):
                total_p = total_p + score[h : h + 8]
                total_n = total_n + w[h : h + 8]
        count = jnp.sum(total_n, axis=0, keepdims=True)
        acc_n[pl.ds(b, 1), lanes] = count
        acc_p[pl.ds(b, 1), lanes] = 0.5 * count + 0.125 * jnp.sum(total_p, axis=0, keepdims=True)

    features = single_ref[0].astype(jnp.float32)
    average = jnp.mean(features, axis=-1, keepdims=True)
    centred = features - average
    variance = jnp.mean(centred * centred, axis=-1, keepdims=True)
    normed = (centred * lax.rsqrt(variance + 1e-05) * gain_ref[...]).astype(jnp.bfloat16)
    first = jnp.maximum(
        jnp.dot(normed, wh_ref[...], preferred_element_type=jnp.float32) + bh_ref[...], 0.0
    ).astype(jnp.bfloat16)
    second = jnp.maximum(
        jnp.dot(first, wm_ref[...], preferred_element_type=jnp.float32) + bm_ref[...], 0.0
    ).astype(jnp.bfloat16)
    logits = (
        lax.dot_general(wl_ref[...], second, (((1,), (1,)), ((), ())), preferred_element_type=jnp.float32)
        + bl_ref[...]
    )
    logits_ref[0] = logits
    total_ref[pl.ds(b, 1), :] = jnp.log(jnp.sum(jnp.exp(logits), axis=0, keepdims=True))

    @pl.when(b == batch - 1)
    def _():
        count = acc_p.shape[0]
        for s in range(C):
            lanes = slice(s * own_len, (s + 1) * own_len)
            parts_ref[s, 0:count, :] = acc_p[:, lanes]
            parts_ref[s, count:, :] = acc_n[:, lanes]


def pairs(rows, cols, neighbor, single, gain, wh, bh, wm, bm, wl, bl, R, C):
    batch, cols_len, rows_len = neighbor.shape
    own_len = rows.shape[3]
    bins = wl.shape[0]
    whole = pl.BlockSpec(memory_space=pltpu.VMEM)
    return pl.pallas_call(
        functools.partial(pair_kernel, R, C, 16),
        grid=(batch,),
        in_specs=[
            whole,
            whole,
            pl.BlockSpec((1, cols_len, rows_len), lambda i: (i, 0, 0)),
            pl.BlockSpec((1,) + single.shape[1:], lambda i: (i, 0, 0)),
        ]
        + [whole] * 7,
        out_specs=[
            pl.BlockSpec((C, 2 * batch, own_len), lambda i: (0, 0, 0)),
            pl.BlockSpec((1, bins, own_len), lambda i: (i, 0, 0)),
            pl.BlockSpec((batch, own_len), lambda i: (0, 0)),
        ],
        out_shape=[
            jax.ShapeDtypeStruct((C, 2 * batch, own_len), jnp.float32),
            jax.ShapeDtypeStruct((batch, bins, own_len), jnp.float32),
            jax.ShapeDtypeStruct((batch, own_len), jnp.float32),
        ],
        scratch_shapes=[
            pltpu.VMEM((cols_len, 64), jnp.bfloat16),
            pltpu.VMEM((cols_len, 64), jnp.bfloat16),
            pltpu.VMEM((64, rows_len), jnp.bfloat16),
            pltpu.VMEM((2, cols_len, 256), jnp.float32),
            pltpu.VMEM((2, cols_len, 256), jnp.float32),
            pltpu.VMEM((batch, rows_len), jnp.float32),
            pltpu.VMEM((batch, rows_len), jnp.float32),
        ],
        compiler_params=pltpu.CompilerParams(dimension_semantics=("arbitrary",)),
        name="pairs",
    )(rows, cols, neighbor, single, gain, wh, bh, wm, bm, wl, bl)


def finish_kernel(
    R, C,
    parts_ref, logits_ref, total_ref, valid_ref,
    lddt_ref, loss_ref, mean_ref,
    landed, tile, mid, tiles_c, tiles_r,
    send_sem, recv_sem, csend_sem, crecv_sem, rsend_sem, rrecv_sem,
):
    r = lax.axis_index("row")
    c = lax.axis_index("col")
    barrier = pltpu.get_barrier_semaphore()
    for k in range(1, C):
        pl.semaphore_signal(barrier, inc=1, device_id=(r, (c + k) % C), device_id_type=MESH)
    for k in range(1, R):
        pl.semaphore_signal(barrier, inc=1, device_id=((r + k) % R, c), device_id_type=MESH)
    pl.semaphore_wait(barrier, C + R - 2)

    copies = []
    for k in range(1, C):
        peer = (c + k) % C
        copy = pltpu.make_async_remote_copy(
            src_ref=parts_ref.at[peer],
            dst_ref=landed.at[k],
            send_sem=send_sem.at[k],
            recv_sem=recv_sem.at[k],
            device_id=(r, peer),
            device_id_type=MESH,
        )
        copy.start()
        copies.append(copy)
    sums = parts_ref[c]
    for copy in copies:
        copy.wait()
    for k in range(1, C):
        sums = sums + landed[k]
    batch = valid_ref.shape[0]
    valid = valid_ref[...]
    lddt = valid * sums[0:batch] / jnp.maximum(valid * sums[batch:], 1.0)
    lddt_ref[...] = lddt
    bins = logits_ref.shape[1]
    logits = logits_ref[...]
    centers = (lax.broadcasted_iota(jnp.int32, logits.shape, 1).astype(jnp.float32) + 0.5) / bins
    apart = lddt[:, None, :] - centers
    closeness = jnp.exp(-(apart * apart) * (bins * bins * 0.5))
    expected = jnp.sum(closeness * logits, axis=1) / jnp.sum(closeness, axis=1)
    loss = valid * (total_ref[...] - expected)
    own_len = valid.shape[1]
    tile[...] = jnp.zeros_like(tile)
    tile[0:1, 0:own_len] = jnp.sum(loss, axis=0, keepdims=True)
    tile[1:2, 0:own_len] = jnp.sum(valid, axis=0, keepdims=True)
    loss_ref[...] = loss

    copies = []
    for k in range(1, C):
        copy = pltpu.make_async_remote_copy(
            src_ref=tile,
            dst_ref=tiles_c.at[c],
            send_sem=csend_sem.at[k],
            recv_sem=crecv_sem.at[k],
            device_id=(r, (c + k) % C),
            device_id_type=MESH,
        )
        copy.start()
        copies.append(copy)
    for copy in copies:
        copy.wait()
    tiles_c[c] = tile[...]
    summed = tiles_c[0]
    for k in range(1, C):
        summed = summed + tiles_c[k]
    mid[...] = summed
    copies = []
    for k in range(1, R):
        copy = pltpu.make_async_remote_copy(
            src_ref=mid,
            dst_ref=tiles_r.at[r],
            send_sem=rsend_sem.at[k],
            recv_sem=rrecv_sem.at[k],
            device_id=((r + k) % R, c),
            device_id_type=MESH,
        )
        copy.start()
        copies.append(copy)
    for copy in copies:
        copy.wait()
    tiles_r[r] = mid[...]
    final = tiles_r[0]
    for k in range(1, R):
        final = final + tiles_r[k]
    both = jnp.sum(final, axis=1, keepdims=True)
    mean_ref[...] = jnp.broadcast_to(both[0:1] / both[1:2], mean_ref.shape)


def finish(parts, logits, total, valid, R, C):
    own = valid.shape
    vmem = pl.BlockSpec(memory_space=pltpu.VMEM)
    return pl.pallas_call(
        functools.partial(finish_kernel, R, C),
        out_shape=(
            jax.ShapeDtypeStruct(own, jnp.float32),
            jax.ShapeDtypeStruct(own, jnp.float32),
            jax.ShapeDtypeStruct((8, 128), jnp.float32),
        ),
        in_specs=[vmem] * 4,
        out_specs=[vmem] * 3,
        scratch_shapes=[
            pltpu.VMEM(parts.shape, jnp.float32),
            pltpu.VMEM((8, 128), jnp.float32),
            pltpu.VMEM((8, 128), jnp.float32),
            pltpu.VMEM((C, 8, 128), jnp.float32),
            pltpu.VMEM((R, 8, 128), jnp.float32),
            pltpu.SemaphoreType.DMA((C,)),
            pltpu.SemaphoreType.DMA((C,)),
            pltpu.SemaphoreType.DMA((C,)),
            pltpu.SemaphoreType.DMA((C,)),
            pltpu.SemaphoreType.DMA((R,)),
            pltpu.SemaphoreType.DMA((R,)),
        ],
        compiler_params=pltpu.CompilerParams(collective_id=1, has_side_effects=True),
        name="finish",
    )(parts, logits, total, valid)


def local(
    R, C,
    neighbor,
    true_coords,
    pred_coords,
    residue_mask,
    single,
    ln_gain,
    w_hidden,
    b_hidden,
    w_mid,
    b_mid,
    w_logits,
    b_logits,
):
    valid = residue_mask.astype(jnp.float32)
    stacked = jnp.concatenate(
        [true_coords, pred_coords, valid[:, None, :], jnp.zeros_like(valid)[:, None, :]], axis=1
    )
    rows, cols = gather(stacked, R, C)
    parts, logits, total = pairs(
        rows,
        cols,
        neighbor,
        single,
        ln_gain[None, :],
        w_hidden,
        b_hidden[None, :],
        w_mid,
        b_mid[None, :],
        w_logits.T,
        b_logits[:, None],
        R,
        C,
    )
    lddt_score, residue_loss, mean = finish(parts, logits, total, valid, R, C)
    return (lddt_score, residue_loss, mean[0, 0])


def solution(mesh):
    R = mesh.shape["row"]
    C = mesh.shape["col"]
    both = P(None, ("row", "col"))
    placed = (
        P(None, "col", "row"),
        P(None, None, ("row", "col")),
        P(None, None, ("row", "col")),
        both,
        P(None, ("row", "col"), None),
        P(),
        P(),
        P(),
        P(),
        P(),
        P(),
        P(),
    )
    return jax.shard_map(
        functools.partial(local, R, C),
        mesh=mesh,
        in_specs=placed,
        out_specs=(both, both, P()),
        check_vma=False,
    )
```

time: 314 us -> 116 us (0.37)
  other arithmetic: 109 us -> 1.44 us
  Pallas kernels: 0 us -> 105 us
  waiting for transfers between devices: 102 us -> 0 us
  blocking collectives: 60.8 us -> 0 us
  between operations: 16.6 us -> 0.66 us
  local copies, waits for them, and re-layouts: 19.7 us -> 8.16 us
  matrix products: 4.59 us -> 0 us
    reduce_sum x4 -> x0, other arithmetic: 105 us -> none  [the longest x1 98.8 us: local(): preserved = jnp.sum(weights * scores, axis=1)]
    pallas_call x0 -> x3, Pallas kernels: none -> 105 us  [the longest x1 61.3 us: pairs(): pl.pallas_call(functools.partial(pair_kernel, R, C, 16), grid=(batch,), i...]
    psum x2 -> x0, waiting for transfers between devices: 101 us -> none  [the longest x1 53.1 us: local(): preserved_all, neighbors_all = lax.psum((preserved, neighbors), 'col')]
    psum x1 -> x0, blocking collectives: 39.6 us -> none  [local(): lax.psum((jnp.sum(residue_loss), jnp.sum(valid)), ('row', 'col'))]
    all_gather x1 -> x0, blocking collectives: 21.3 us -> none  [local(): rows_part = lax.all_gather(stacked, 'col', axis=2, tiled=True)]
    slice x2 -> x1, local copies, waits for them, and re-layouts: 10 us -> 1.19 us  [local(): return (lddt_score, residue_loss, mean[0, 0])]
    sub x12 -> x0, local copies, waits for them, and re-layouts: 7.5 us -> none  [the longest x4 2.5 us: tile_dist(): total = total + (cols_block[:, 2, :, None] - rows_block[:, 2, None, :]) ** 2]
    dot_general x2 -> x0, matrix products: 4.59 us -> none  [the longest x1 3.15 us: head_loss(): jnp.dot(first_hidden, w_mid, preferred_element_type=jnp.float32) + b_mid]
  transfers between devices with their start and end apart: 2 -> 0, of which waited for: 2 -> 0; matrix products, arithmetic and copies ran while one was open for 7% -> 0% of each run, Pallas kernels for 0% -> 0%
where the time goes in v1:
time: 116 us; the launch traced here: 115 us
  Pallas kernels  105 us (91%)
  local copies, waits for them, and re-layouts  8.16 us (7%)
  other arithmetic  1.44 us (1%)
    pallas_call x1, Pallas kernels, pairs(): pl.pallas_call(functools.partial(pair_kernel, R, C, 16), grid=(batch,), i...  61.3 us
    pallas_call x1, Pallas kernels, gather(): pl.pallas_call(functools.partial(gather_kernel, R, C), out_shape=(jax.Sha...  26.2 us
    pallas_call x1, Pallas kernels, finish(): pl.pallas_call(functools.partial(finish_kernel, R, C), out_shape=(jax.Sha...  17.4 us
    unnamed x6, local copies, waits for them, and re-layouts  4.32 us

profile of v1, /device:TPU:0, one launch (start us, length us, event | category | flops | bytes accessed | tf_op | source)
XLA Modules:
  0.0 115.1 jit_solution(12334561213341659906)
XLA Ops:
  0.6 0.1 pad.3.clone
  0.7 1.2 %broadcast_in_dim.16.gain_ref = f32[1,384]{1,0:T(1,128)} reshape(f32[384]{0:T(512)} %param.17) | data formatting | bytes 3072 | tf_op jit(solution)/shard_map/broadcast_in_dim | solution.py:415
  1.9 0.7 convert_element_type.3.valid_ref
  2.6 0.0 copy-start
  2.6 1.4 %copy.18.bl_ref = f32[50,1]{1,0:T(8,128)} copy(f32[50,1]{0,1:T(1,128)} %bitcast.11) | data formatting | bytes 400 | tf_op jit(solution)/shard_map/broadcast_in_dim | solution.py:421
  4.0 0.8 copy.15
  4.8 0.8 copy.16
  5.7 0.7 maximum_maximum_fusion.x_ref
  6.4 26.2 %gather.1 = (f32[8,32,8,96]{3,2,1,0:T(8,128)}, f32[4,32,8,96]{3,2,1,0:T(8,128)}) custom-call(f32[32,8,96]{2,1,0:T(8,128)} %maximum_maximum_fusion.x_ref), custom_call_target="tpu_custom_call" | custom-call | tf_op jit(solution)/shard_map/gather/pallas_call | solution.py:104
  32.6 61.3 %pairs.1 = (f32[8,64,96]{2,1,0:T(8,128)}, f32[32,50,96]{2,1,0:T(8,128)}, f32[32,96]{1,0:T(8,128)}) custom-call(f32[8,32,8,96]{3,2,1,0:T(8,128)} %get-tuple-element.11.rows_ref, f32[4,32,8,96]{3,2,1,0:T(8,128)} %get-tuple-element.12.cols_ref, s32[32,384,768]{2,1,0:T(8,128)} %neighbor_ref.1, bf16[32,96,384]{2,1,0:T(8,128)(2,1)} %single_ref.1, ...), custom_call_target="tpu_custom_call" | custom-call | tf_op jit(solution)/shard_map/pairs/pallas_call | solution.py:234
  93.9 0.0 copy-done
  93.9 17.4 %finish.1 = (f32[32,96]{1,0:T(8,128)}, f32[32,96]{1,0:T(8,128)}, f32[8,128]{1,0:T(8,128)}) custom-call(f32[8,64,96]{2,1,0:T(8,128)} %get-tuple-element.13.parts_ref, f32[32,50,96]{2,1,0:T(8,128)} %get-tuple-element.14.logits_ref, f32[32,96]{1,0:T(8,128)} %get-tuple-element.15.total_ref, f32[32,96]{1,0:T(8,128)} %copy-done), custom_call_target="tpu_custom_call" | custom-call | tf_op jit(solution)/shard_map/finish/pallas_call | solution.py:363
  111.3 1.2 %slice.3 = f32[1,1]{1,0:T(1,128)} slice(f32[8,128]{1,0:T(8,128)} %get-tuple-element.18), slice={[0:1], [0:1]} | slice | bytes 8 | tf_op jit(solution)/shard_map/slice | solution.py:426
  112.5 1.3 %copy.21 = f32[32,96]{1,0:T(8,128)} copy(f32[32,96]{1,0:T(8,128)} %get-tuple-element.22) | data formatting | bytes 24576
  113.8 1.3 %copy.22 = f32[32,96]{1,0:T(8,128)} copy(f32[32,96]{1,0:T(8,128)} %get-tuple-element.23) | data formatting | bytes 24576
Async XLA Ops:
  2.6 91.3 %copy-start = (f32[32,96]{1,0:T(8,128)}, f32[32,96]{1,0:T(8,128)S(1)}, u32[]{:S(2)}) copy-start(f32[32,96]{1,0:T(8,128)S(1)} %convert_element_type.3.valid_ref) | copy-start | bytes 36868
